TPU v7x, 32 devices: a whole 2x2x4 slice. The times are simulated.
32 devices in a mesh: tm: 8 (over z, y), freq: 4 (over x, core).
Axes of the slice: x: 2, y: 2, z: 4, core: 2. Of those that a mesh axis runs over, the one named last changes fastest.
Arguments:
- snapshots: bfloat16 [4352, 3, 4096], P('tm', None, 'freq'), may hold values from -200 to 200
- block_starts: int32 [32], replicated, may hold values from 0 to 4032, as said below
- freq_index: int32 [16], replicated, may hold values from 0 to 128
Outputs:
- modes: bfloat16 [16, 32, 2, 3, 4096], P(None, None, None, None, ('freq', 'tm'))
- energy: float32 [16], replicated
Inputs may be any that keep to these rules, and one draw needn't show every extreme that they name: `block_starts`: block b starts at b * 128 plus between 0 and 64.
All inputs are finite; a program needn't handle non-finite values.
Results may differ from a plain program's by a relative error of at most 0.0085.
Values may be sent and summed in bfloat16 or wider, within the bound.
A program may use at most 64 MiB of HBM per device.

v0:
```python
import math
import jax
import jax.numpy as jnp
from jax import lax
from jax.sharding import PartitionSpec as P

NB = 32
NFFT = 256
NF = 16
NSIT = 6


def for_sending(shard):
    return jax.tree.map(lambda a: a.astype(jnp.bfloat16) if a.dtype == jnp.float32 else a, shard)


def dft_rows(freq_index):
    times_idx = jnp.arange(NFFT, dtype=jnp.int32)
    phase_int = freq_index[:, None] * times_idx[None, :] % NFFT
    angles = 2.0 * math.pi / NFFT * phase_int.astype(jnp.float32)
    window = 0.5 - 0.5 * jnp.cos(2.0 * math.pi / NFFT * times_idx.astype(jnp.float32))
    scaling = 1.0 / jnp.sqrt(jnp.sum(window * window))
    cosine = window[None, :] * jnp.cos(angles) * scaling
    sine_rows = -window[None, :] * jnp.sin(angles) * scaling
    return jnp.stack([cosine, sine_rows], 1).reshape(2 * NF, NFFT).astype(jnp.bfloat16)


def block_rows(block_starts):
    return block_starts[:, None] + jnp.arange(NFFT, dtype=jnp.int32)[None, :]


def matmul_batch(left, right):
    return jnp.einsum("fij,fjk->fik", left, right, precision=lax.Precision.HIGHEST)


def whiten(summed, points):
    gram_re = summed[:, 0]
    gram_im = summed[:, 1]
    top_rows = jnp.concatenate([gram_re, -gram_im], 2)
    low_rows = jnp.concatenate([gram_im, gram_re], 2)
    hermit = jnp.concatenate([top_rows, low_rows], 1)
    frob = jnp.sqrt(jnp.sum(hermit * hermit, axis=(1, 2)) + 1e-06)
    identity = jnp.eye(2 * NB, dtype=jnp.float32)[None]
    iterate = hermit / frob[:, None, None]
    inverse = jnp.broadcast_to(identity, hermit.shape)
    for iteration in range(NSIT):
        factor = 1.5 * identity - 0.5 * matmul_batch(inverse, iterate)
        iterate = matmul_batch(iterate, factor)
        inverse = matmul_batch(factor, inverse)
    columns = inverse[:, :, :NB] * jnp.sqrt(6.0 * points / frob)[:, None, None]
    upper = columns[:, :NB]
    lower = columns[:, NB:]
    coefficients = jnp.stack([jnp.stack([upper, -lower], 1), jnp.stack([lower, upper], 1)], 1)
    energy = jnp.trace(gram_re, axis1=1, axis2=2) / (3.0 * NB * points)
    return (coefficients, energy)


def local(snapshots, block_starts, freq_index):
    dft_table = dft_rows(freq_index)
    offsets = block_rows(block_starts)
    series = lax.all_to_all(snapshots, "tm", split_axis=2, concat_axis=0, tiled=True)
    count = series.shape[1]
    width = series.shape[2]
    columns_all = series.reshape(series.shape[0], count * width)
    windows = jnp.take(columns_all, offsets, axis=0)
    spectra_part = jnp.einsum(
        "rt,btn->rbn", dft_table, windows, preferred_element_type=jnp.float32
    ).astype(jnp.bfloat16)
    spectra = spectra_part.reshape(2 * NF, NB, count, width)
    width = spectra.shape[3]
    points = float(width * lax.axis_size("tm") * lax.axis_size("freq"))
    flat_spec = spectra.reshape(NF, 2, NB, 3 * width)
    real_part = flat_spec[:, 0]
    imag_part = flat_spec[:, 1]
    gram_re = jnp.einsum("fbn,fcn->fbc", real_part, real_part, preferred_element_type=jnp.float32)
    gram_re = gram_re + jnp.einsum(
        "fbn,fcn->fbc", imag_part, imag_part, preferred_element_type=jnp.float32
    )
    cross_terms = jnp.einsum(
        "fbn,fcn->fbc", real_part, imag_part, preferred_element_type=jnp.float32
    )
    partial_gram = jnp.stack([gram_re, cross_terms - jnp.swapaxes(cross_terms, 1, 2)], 1)
    shared = lax.psum_scatter(partial_gram, "freq", scatter_dimension=0, tiled=True)
    shared = lax.psum(shared, "tm")
    coef_part, energy_part = whiten(shared, points)
    coefficients, energy = (
        lax.all_gather(for_sending(coef_part), "freq", axis=0, tiled=True).astype(coef_part.dtype),
        lax.all_gather(for_sending(energy_part), "freq", axis=0, tiled=True).astype(
            energy_part.dtype
        ),
    )
    coef_bf = jnp.transpose(coefficients.astype(jnp.bfloat16), (0, 4, 1, 2, 3))
    modes = jnp.einsum(
        "fjorb,frbn->fjon", coef_bf, flat_spec, preferred_element_type=jnp.float32
    ).astype(jnp.bfloat16)
    return (modes.reshape(NF, NB, 2, 3, width), energy)


def solution(mesh):
    return jax.shard_map(
        local,
        mesh=mesh,
        in_specs=(P("tm", None, "freq"), P(), P()),
        out_specs=(P(None, None, None, None, ("freq", "tm")), P()),
        check_vma=False,
    )
```

profile of v0, /device:TPU:0, one launch (start us, length us, event | category | flops | bytes accessed | tf_op | source)
XLA Modules:
  0.0 302.0 jit_solution(5454978820925684729)
XLA Ops:
  7.2 8.6 %copy.43 = bf16[544,3,1024]{0,1,2:T(4,128)(2,1)} copy(bf16[544,3,1024]{2,0,1:T(8,128)(2,1)} %param.3) | data formatting | bytes 6684672 | tf_op args[0]
  15.8 0.0 copy-start.2
  15.8 0.0 copy-start
  15.8 0.0 copy-start.1
  15.8 7.4 %all-to-all-start = ((bf16[544,3,1024]{0,1,2:T(4,128)(2,1)}), bf16[544,3,1024]{0,1,2:T(4,128)(2,1)}, u32[]{:S(2)}, u32[]{:S(2)}) async-start(bf16[544,3,1024]{0,1,2:T(4,128)(2,1)} %copy.43), calls=%async_computation | async-start | bytes 10485760 | tf_op jit(solution)/shard_map/all_to_all | solution.py:61
  23.2 0.0 all-reduce.4.cloned.1.call-start
  23.3 0.6 multiply_reduce_fusion.1
  24.7 0.0 copy-done.2
  24.7 0.2 multiply_convert_fusion.1
  24.9 0.0 copy-done
  24.9 0.1 fusion.26
  25.0 0.0 copy-done.1
  25.0 0.6 fusion.43
  27.0 0.1 fusion.31
  27.1 111.9 %all-to-all-done = bf16[544,3,1024]{0,1,2:T(4,128)(2,1)} async-done(((bf16[544,3,1024]{0,1,2:T(4,128)(2,1)}), bf16[544,3,1024]{0,1,2:T(4,128)(2,1)}, u32[]{:S(2)}, u32[]{:S(2)}) %all-to-all-start) | async-done | bytes 3342368 | tf_op jit(solution)/shard_map/all_to_all | solution.py:61
  139.0 7.4 %copy.74 = bf16[544,3,8,128]{0,2,3,1:T(8,128)(2,1)} copy(bf16[544,3,8,128]{0,1,3,2:T(4,128)(2,1)} %bitcast) | data formatting | bytes 6684672 | tf_op jit(solution)/shard_map/all_to_all | solution.py:61
  146.4 7.4 %reshape.243 = bf16[4352,384]{0,1:T(8,128)(2,1)} reshape(bf16[8,544,3,128]{1,0,3,2:T(8,128)(2,1)} %bitcast.97) | data formatting | bytes 6684672 | tf_op jit(solution)/shard_map/reshape | solution.py:64
  153.7 5.6 %copy.45 = bf16[4352,384]{1,0:T(8,128)(2,1)S(1)} copy(bf16[4352,384]{0,1:T(8,128)(2,1)} %reshape.243) | data formatting | bytes 6684672 | tf_op jit(solution)/shard_map/reshape | solution.py:64
  159.4 33.1 %gather_fusion = bf16[8192,384]{1,0:T(8,128)(2,1)} fusion(bf16[4352,384]{1,0:T(8,128)(2,1)S(1)} %copy.45, s32[8192]{0:T(1024)S(1)} %broadcast_clamp_fusion), kind=kCustom, calls=%fused_computation | custom fusion | bytes 12615680 | tf_op jit(solution)/shard_map/jit(_take)/gather | solution.py:65
  192.5 4.6 %fusion.4 = bf16[32,32,384]{2,0,1:T(8,128)(2,1)S(1)} fusion(bf16[32,256,1]{1,0,2:T(8,128)(2,1)S(1)} %reshape.260, bf16[32,256,384]{2,1,0:T(8,128)(2,1)} %bitcast.99, pred[32,256]{1,0:T(8,128)(4,1)S(1)} %fusion.31), kind=kOutput, calls=%fused_computation.7 | convolution fusion | flops 204865536 | bytes 7102464 | tf_op jit(solution)/shard_map/rt,btn->rbn/dot_general | solution.py:66
  197.1 0.3 reshape_reshape.3
  197.4 1.1 fusion.42
  198.5 0.3 fusion.18
  198.8 0.5 fusion.17
  199.4 0.1 copy.48
  199.6 0.3 fusion.7
  199.9 0.8 pad_maximum_fusion
  200.7 0.0 all-reduce.4.cloned.1.call-update
  200.8 32.6 %all-reduce.4.cloned.1.call-done = f32[16,2,32,32]{3,2,0,1:T(8,128)} async-done(((f32[16,2,32,32]{3,2,0,1:T(8,128)}), f32[16,2,32,32]{3,2,0,1:T(8,128)}) %all-reduce.4.cloned.1.call-update) | async-done | bytes 131088
  233.4 0.9 constant_dynamic-slice_fusion
  234.3 38.6 %psum.7 = f32[4,2,32,32]{3,2,0,1:T(8,128)S(1)} all-reduce(f32[4,2,32,32]{3,2,0,1:T(8,128)S(1)} %constant_dynamic-slice_fusion), channel_id=1, replica_groups=mesh['tm'=8,'freq'=4] {'tm'}, use_global_device_ids=true, to_apply=%region_2.3 | all-reduce | flops 8192 | bytes 65536 | tf_op jit(solution)/shard_map/psum | solution.py:84
  273.0 0.1 select_reduce_fusion
  273.1 0.2 multiply_reduce_fusion
  273.3 0.4 fusion.13
  273.7 0.3 fusion.41
  274.0 0.3 fusion.20
  274.2 0.3 fusion.12
  274.5 0.3 fusion.45
  274.8 0.3 fusion.44
  275.0 0.3 fusion.11
  275.3 0.3 fusion.47
  275.6 0.3 fusion.46
  275.8 0.3 fusion.10
  276.1 0.3 fusion.49
  276.3 0.3 fusion.48
  276.6 0.3 fusion.9
  276.9 0.3 fusion.51
  277.1 0.3 fusion.50
  277.4 0.3 fusion.8
  277.7 0.4 convolution_multiply_fusion.6
  278.0 0.1 fusion.23
  278.1 0.1 fusion.24
  278.3 6.5 %all_gather.6 = bf16[16,2,2,32,32]{3,4,0,2,1:T(8,128)(2,1)S(1)} all-gather(bf16[4,2,2,32,32]{3,4,0,2,1:T(8,128)(2,1)S(1)} %pad_maximum_fusion.1), channel_id=1, replica_groups=mesh['tm'=8,'freq'=4] {'freq'}, dimensions={0}, use_global_device_ids=true | all-gather | bytes 163840 | tf_op jit(solution)/shard_map/all_gather | solution.py:87
  284.8 0.4 bitcast_convert_fusion
  285.2 0.3 reshape.244
  285.5 0.2 dynamic-update-slice
  285.8 2.1 copy.52
  287.9 6.8 %all-reduce = bf16[16]{0:T(256)(128)(2,1)S(1)} all-reduce(bf16[16]{0:T(256)(128)(2,1)S(1)} %dynamic-update-slice), channel_id=1, replica_groups=mesh['tm'=8,'freq'=4] {'freq'}, use_global_device_ids=true, to_apply=%add | all-reduce | flops 16 | bytes 64
  294.7 0.5 convert_element_type.64
  (16 shorter events, 0.3 us)
Async XLA Ops:
  15.8 8.9 %copy-start.2 = (s32[16]{0:T(128)S(1)}, s32[16]{0:T(128)}, u32[]{:S(2)}) copy-start(s32[16]{0:T(128)} %param.5) | copy-start | bytes 196
  15.8 9.1 %copy-start = (s32[32]{0:T(128)S(1)}, s32[32]{0:T(128)}, u32[]{:S(2)}) copy-start(s32[32]{0:T(128)} %param.4) | copy-start | bytes 388
  15.8 9.2 %copy-start.1 = (u32[32]{0:T(128)S(1)}, u32[32]{0:T(128)}, u32[]{:S(2)}) copy-start(u32[32]{0:T(128)} %constant.55) | copy-start | bytes 388
  15.8 123.2 %all-to-all-start = ((bf16[544,3,1024]{0,1,2:T(4,128)(2,1)}), bf16[544,3,1024]{0,1,2:T(4,128)(2,1)}, u32[]{:S(2)}, u32[]{:S(2)}) async-start(bf16[544,3,1024]{0,1,2:T(4,128)(2,1)} %copy.43), calls=%async_computation | async-start | bytes 10485760 | tf_op jit(solution)/shard_map/all_to_all | solution.py:61
  23.2 210.1 %all-reduce.4.cloned.1.call-start = ((), (), s32[]{:S(2)}) async-start(), calls=%async_computation.1 | async-start | bytes 1048576
Sparse Core Ops, SparseCore 0:
  200.9 32.4 all-reduce.3
where the time goes:
time: 303 us; the launch traced here: 302 us
  waiting for transfers between devices  145 us (48%)
  local copies, waits for them, and re-layouts  67.9 us (22%)
  blocking collectives  51.9 us (17%)
  between operations  16.4 us (5%)
  matrix products  10.8 us (4%)
  starting transfers between devices  7.49 us (2%)
    all_to_all x1, waiting for transfers between devices, local(): lax.all_to_all(snapshots, 'tm', split_axis=2, concat_axis=0, tiled=True)  112 us
    psum x1, blocking collectives, local(): shared = lax.psum(shared, 'tm')  38.6 us
    gather x1, local copies, waits for them, and re-layouts, local(): windows = jnp.take(columns_all, offsets, axis=0)  33.1 us
    unnamed x2, waiting for transfers between devices  32.6 us
    reshape x2, local copies, waits for them, and re-layouts, local(): columns_all = series.reshape(series.shape[0], count * width)  13 us
    unnamed x13, local copies, waits for them, and re-layouts  12.5 us
    all_to_all x1, starting transfers between devices, local(): lax.all_to_all(snapshots, 'tm', split_axis=2, concat_axis=0, tiled=True)  7.45 us
    all_to_all x1, local copies, waits for them, and re-layouts, local(): lax.all_to_all(snapshots, 'tm', split_axis=2, concat_axis=0, tiled=True)  7.37 us
  transfers between devices with their start and end apart: 2, of which 2 were waited for; matrix products, arithmetic and copies ran while one was open for 1% of the time, Pallas kernels for 0%

commit v1 on v0

--- a/solution.py
+++ b/solution.py
@@ -58,7 +58,9 @@
 def local(snapshots, block_starts, freq_index):
     dft_table = dft_rows(freq_index)
     offsets = block_rows(block_starts)
-    series = lax.all_to_all(snapshots, "tm", split_axis=2, concat_axis=0, tiled=True)
+    pieces = jnp.split(snapshots, lax.axis_size("tm"), axis=2)
+    got = lax.all_to_all(jnp.stack(pieces), "tm", 0, 0)
+    series = jnp.concatenate(got, axis=0)
     count = series.shape[1]
     width = series.shape[2]
     columns_all = series.reshape(series.shape[0], count * width)

time: 303 us -> 250 us (0.83)
  waiting for transfers between devices: 145 us -> 104 us
  local copies, waits for them, and re-layouts: 67.9 us -> 56.1 us
    all_to_all x1, waiting for transfers between devices: 112 us -> 71.1 us  [local(): got = lax.all_to_all(jnp.stack(pieces), 'tm', 0, 0)]
    reshape x2 -> x0, local copies, waits for them, and re-layouts: 13 us -> none  [local(): columns_all = series.reshape(series.shape[0], count * width)]
    all_to_all x1 -> x0, local copies, waits for them, and re-layouts: 7.37 us -> none  [local(): lax.all_to_all(snapshots, 'tm', split_axis=2, concat_axis=0, tiled=True)]
    unnamed x13 -> x20, local copies, waits for them, and re-layouts: 12.5 us -> 17 us
    another operation x0 -> x2, local copies, waits for them, and re-layouts: none -> 4.09 us  [the longest x1 2.29 us: local(): columns_all = series.reshape(series.shape[0], count * width)]
where the time goes in v1:
time: 250 us; the launch traced here: 249 us
  waiting for transfers between devices  104 us (42%)
  local copies, waits for them, and re-layouts  56.1 us (22%)
  blocking collectives  51.9 us (21%)
  between operations  16.4 us (7%)
  matrix products  10.8 us (4%)
  starting transfers between devices  7.48 us (3%)
  other arithmetic  2.93 us (1%)
    all_to_all x1, waiting for transfers between devices, local(): got = lax.all_to_all(jnp.stack(pieces), 'tm', 0, 0)  71.1 us
    psum x1, blocking collectives, local(): shared = lax.psum(shared, 'tm')  38.4 us
    gather x1, local copies, waits for them, and re-layouts, local(): windows = jnp.take(columns_all, offsets, axis=0)  33.1 us
    unnamed x2, waiting for transfers between devices  32.6 us
    unnamed x20, local copies, waits for them, and re-layouts  17 us
    all_to_all x1, starting transfers between devices, local(): got = lax.all_to_all(jnp.stack(pieces), 'tm', 0, 0)  7.44 us
    unnamed x1, blocking collectives  6.78 us
    all_gather x1, blocking collectives, local(): lax.all_gather(for_sending(coef_part), 'freq', axis=0, tiled=True)  6.68 us
  transfers between devices with their start and end apart: 2, of which 2 were waited for; matrix products, arithmetic and copies ran while one was open for 1% of the time, Pallas kernels for 0%

profile of v1, /device:TPU:0, one launch (start us, length us, event | category | flops | bytes accessed | tf_op | source)
XLA Modules:
  0.0 249.4 jit_solution(18214542786638048519)
XLA Ops:
  7.2 1.8 bitcast_dynamic-update-slice_fusion.7
  8.9 1.8 bitcast_dynamic-update-slice_fusion.6
  10.7 1.8 bitcast_dynamic-update-slice_fusion.5
  12.5 1.8 bitcast_dynamic-update-slice_fusion.4
  14.3 1.8 bitcast_dynamic-update-slice_fusion.3
  16.1 1.8 bitcast_dynamic-update-slice_fusion.2
  17.9 1.8 bitcast_dynamic-update-slice_fusion.1
  19.7 1.8 bitcast_dynamic-update-slice_fusion
  21.5 0.0 copy-start.2
  21.5 0.0 copy-start
  21.5 7.4 %all-to-all-start = ((bf16[8,544,3,128]{3,1,2,0:T(8,128)(2,1)}), bf16[8,544,3,128]{3,1,2,0:T(8,128)(2,1)S(1)}, u32[]{:S(2)}, u32[]{:S(2)}) async-start(bf16[8,544,3,128]{3,1,2,0:T(8,128)(2,1)} %bitcast_dynamic-update-slice_fusion), calls=%async_computation | async-start | bytes 6684672 | tf_op jit(solution)/shard_map/all_to_all | solution.py:62
  29.0 0.0 all-reduce.4.cloned.1.call-start
  29.0 0.6 multiply_reduce_fusion.1
  30.4 0.0 copy-done.2
  30.4 0.2 multiply_convert_fusion.1
  30.6 0.0 copy-done
  30.6 0.1 fusion.26
  30.7 0.0 copy-done.1
  30.8 0.6 fusion.43
  32.7 0.1 fusion.31
  32.8 71.1 %all-to-all-done = bf16[8,544,3,128]{3,1,2,0:T(8,128)(2,1)S(1)} async-done(((bf16[8,544,3,128]{3,1,2,0:T(8,128)(2,1)}), bf16[8,544,3,128]{3,1,2,0:T(8,128)(2,1)S(1)}, u32[]{:S(2)}, u32[]{:S(2)}) %all-to-all-start) | async-done | bytes 3342368 | tf_op jit(solution)/shard_map/all_to_all | solution.py:62
  103.9 2.3 copy.53
  106.2 0.6 copy.74
  106.8 33.1 %gather_fusion = bf16[8192,384]{1,0:T(8,128)(2,1)} fusion(bf16[4352,384]{1,0:T(8,128)(2,1)S(1)} %bitcast.110, s32[8192]{0:T(1024)S(1)} %broadcast_clamp_fusion), kind=kCustom, calls=%fused_computation | custom fusion | bytes 12615680 | tf_op jit(solution)/shard_map/jit(_take)/gather | solution.py:67
  139.9 4.6 %fusion.4 = bf16[32,32,384]{2,0,1:T(8,128)(2,1)S(1)} fusion(bf16[32,256,1]{1,0,2:T(8,128)(2,1)S(1)} %reshape.255, bf16[32,256,384]{2,1,0:T(8,128)(2,1)} %bitcast.113, pred[32,256]{1,0:T(8,128)(4,1)S(1)} %fusion.31), kind=kOutput, calls=%fused_computation.7 | convolution fusion | flops 204865536 | bytes 7102464 | tf_op jit(solution)/shard_map/rt,btn->rbn/dot_general | solution.py:68
  144.5 0.3 reshape_reshape.7
  144.8 1.1 fusion.42
  145.9 0.3 fusion.18
  146.2 0.5 fusion.17
  146.7 0.1 copy.45
  146.9 0.3 fusion.7
  147.3 0.8 pad_maximum_fusion
  148.1 0.0 all-reduce.4.cloned.1.call-update
  148.2 32.6 %all-reduce.4.cloned.1.call-done = f32[16,2,32,32]{3,2,0,1:T(8,128)} async-done(((f32[16,2,32,32]{3,2,0,1:T(8,128)}), f32[16,2,32,32]{3,2,0,1:T(8,128)}) %all-reduce.4.cloned.1.call-update) | async-done | bytes 131088
  180.8 0.9 constant_dynamic-slice_fusion
  181.7 38.4 %psum.7 = f32[4,2,32,32]{3,2,0,1:T(8,128)S(1)} all-reduce(f32[4,2,32,32]{3,2,0,1:T(8,128)S(1)} %constant_dynamic-slice_fusion), channel_id=1, replica_groups=mesh['tm'=8,'freq'=4] {'tm'}, use_global_device_ids=true, to_apply=%region_2.3 | all-reduce | flops 8192 | bytes 65536 | tf_op jit(solution)/shard_map/psum | solution.py:86
  220.2 0.1 select_reduce_fusion
  220.3 0.2 multiply_reduce_fusion
  220.5 0.4 fusion.13
  220.9 0.3 fusion.41
  221.2 0.3 fusion.20
  221.4 0.3 fusion.12
  221.7 0.3 fusion.45
  222.0 0.3 fusion.44
  222.2 0.3 fusion.11
  222.5 0.3 fusion.47
  222.8 0.3 fusion.46
  223.0 0.3 fusion.10
  223.3 0.3 fusion.49
  223.6 0.3 fusion.48
  223.8 0.3 fusion.9
  224.1 0.3 fusion.51
  224.3 0.3 fusion.50
  224.6 0.3 fusion.8
  224.9 0.4 convolution_multiply_fusion.6
  225.2 0.1 fusion.23
  225.3 0.1 fusion.24
  225.5 6.7 %all_gather.6 = bf16[16,2,2,32,32]{3,4,0,2,1:T(8,128)(2,1)S(1)} all-gather(bf16[4,2,2,32,32]{3,4,0,2,1:T(8,128)(2,1)S(1)} %pad_maximum_fusion.1), channel_id=1, replica_groups=mesh['tm'=8,'freq'=4] {'freq'}, dimensions={0}, use_global_device_ids=true | all-gather | bytes 163840 | tf_op jit(solution)/shard_map/all_gather | solution.py:89
  232.2 0.4 bitcast_convert_fusion
  232.6 0.3 reshape.239
  232.9 0.2 dynamic-update-slice
  233.2 2.1 copy.49
  235.3 6.8 %all-reduce = bf16[16]{0:T(256)(128)(2,1)S(1)} all-reduce(bf16[16]{0:T(256)(128)(2,1)S(1)} %dynamic-update-slice), channel_id=1, replica_groups=mesh['tm'=8,'freq'=4] {'freq'}, use_global_device_ids=true, to_apply=%add | all-reduce | flops 16 | bytes 64
  242.0 0.5 convert_element_type.64
  (17 shorter events, 0.3 us)
Async XLA Ops:
  21.5 8.9 %copy-start.2 = (s32[16]{0:T(128)S(1)}, s32[16]{0:T(128)}, u32[]{:S(2)}) copy-start(s32[16]{0:T(128)} %param.5) | copy-start | bytes 196
  21.5 9.1 %copy-start = (s32[32]{0:T(128)S(1)}, s32[32]{0:T(128)}, u32[]{:S(2)}) copy-start(s32[32]{0:T(128)} %param.4) | copy-start | bytes 388
  21.5 9.2 %copy-start.1 = (u32[32]{0:T(128)S(1)}, u32[32]{0:T(128)}, u32[]{:S(2)}) copy-start(u32[32]{0:T(128)} %constant.55) | copy-start | bytes 388
  21.5 82.4 %all-to-all-start = ((bf16[8,544,3,128]{3,1,2,0:T(8,128)(2,1)}), bf16[8,544,3,128]{3,1,2,0:T(8,128)(2,1)S(1)}, u32[]{:S(2)}, u32[]{:S(2)}) async-start(bf16[8,544,3,128]{3,1,2,0:T(8,128)(2,1)} %bitcast_dynamic-update-slice_fusion), calls=%async_computation | async-start | bytes 6684672 | tf_op jit(solution)/shard_map/all_to_all | solution.py:62
  29.0 151.8 %all-reduce.4.cloned.1.call-start = ((), (), s32[]{:S(2)}) async-start(), calls=%async_computation.1 | async-start | bytes 1048576
Sparse Core Ops, SparseCore 0:
  148.3 32.4 all-reduce.3
